TPU v7x, 32 devices: a whole 2x2x4 slice. The times are simulated.
32 devices in a mesh: rows: 8 (over z, x), cols: 4 (over y, core).
Axes of the slice: x: 2, y: 2, z: 4, core: 2. Of those that a mesh axis runs over, the one named last changes fastest.
Arguments:
- matrix: float32 [512, 32, 2, 128], P('rows', 'cols'), may hold values from -54 to 54
- plan: int32 [2, 4, 256], replicated, may hold values from 0 to 255, as said below
Outputs:
- rotated: float32 [512, 32, 2, 128], P('rows', 'cols')
Inputs may be any that keep to these rules, and one draw needn't show every extreme that they name: Each plan[s, r] pairs the 256 columns: partner of partner of i is i, and no column is its own partner.
All inputs are finite; a program needn't handle non-finite values.
Results may differ from a plain program's by a relative error of at most 0.0003.
Values sent between devices are 32-bit elements; how exact they have to be, the bound alone decides.
A program may use at most 128 MiB of HBM per device.

v0:
```python
import jax
import jax.numpy as jnp
from jax import lax
from jax.sharding import PartitionSpec as P

STEPS = 2


def passed_along(block, axis, distance):
    devices = range(lax.axis_size(axis))
    route = [((i - distance) % len(devices), i) for i in devices]
    return lax.ppermute(block, axis, route)


def diagonalize(grams, table):
    width = grams.shape[1]
    indices = jnp.arange(width, dtype=jnp.int32)
    rotation = jnp.broadcast_to(jnp.eye(width, dtype=jnp.float32), grams.shape)
    unit_matrix = jnp.eye(width, dtype=jnp.float32)
    for round_index in range(table.shape[0]):
        partner = table[round_index]
        onehot = (partner[:, None] == indices[None, :]).astype(jnp.float32)
        diagonal_now = jnp.diagonal(grams, axis1=1, axis2=2)
        partner_diag = jnp.einsum(
            "pj,ij->pi", diagonal_now, onehot, precision=lax.Precision.HIGHEST
        )
        partner_gram = jnp.sum(grams * onehot[None], axis=2)
        orient = jnp.where(indices < partner, 1.0, -1.0).astype(jnp.float32)
        spread = orient[None, :] * (partner_diag - diagonal_now)
        sign_part = jnp.where(spread >= 0.0, 1.0, -1.0).astype(jnp.float32)
        tangent = (
            sign_part
            * 2.0
            * partner_gram
            / (jnp.abs(spread) + jnp.sqrt(spread * spread + 4.0 * partner_gram * partner_gram))
        )
        cosine = 1.0 / jnp.sqrt(1.0 + tangent * tangent)
        sine_part = tangent * cosine
        off_part = jnp.swapaxes(onehot[None] * (-orient[None, :] * sine_part)[:, :, None], 1, 2)
        rot_now = cosine[:, :, None] * unit_matrix[None] + off_part
        product = jnp.einsum("pij,pjk->pik", grams, rot_now, precision=lax.Precision.HIGHEST)
        grams = jnp.einsum("pji,pjk->pik", rot_now, product, precision=lax.Precision.HIGHEST)
        rotation = jnp.einsum("pij,pjk->pik", rotation, rot_now, precision=lax.Precision.HIGHEST)
    return (grams, rotation)


def full_grams(columns):
    local_sum = jnp.einsum("mpi,mpj->pij", columns, columns, precision=lax.Precision.HIGHEST)
    return lax.psum(local_sum, "rows")


def body(matrix, plan):
    rows_here, pair_here, halves, width = matrix.shape
    columns = matrix.reshape(rows_here, pair_here, halves * width)
    grams = full_grams(columns)
    for step_index in range(STEPS):
        grams, rotation = diagonalize(grams, plan[step_index])
        columns = jnp.einsum("mpi,pij->mpj", columns, rotation, precision=lax.Precision.HIGHEST)
        quarter = columns.reshape(rows_here, pair_here, halves, width)
        tops = quarter[:, :, 0, :]
        bottoms = quarter[:, :, 1, :]
        bottoms, low_grams = passed_along((bottoms, grams[:, width:, width:]), "cols", 1)
        columns = jnp.stack([tops, bottoms], axis=2).reshape(rows_here, pair_here, halves * width)
        if step_index + 1 < STEPS:
            cross_local = jnp.einsum("mpi,mpj->pij", tops, bottoms, precision=lax.Precision.HIGHEST)
            cross = lax.psum(cross_local, "rows")
            upper_rows = jnp.concatenate([grams[:, :width, :width], cross], axis=2)
            lower_rows = jnp.concatenate([jnp.swapaxes(cross, 1, 2), low_grams], axis=2)
            grams = jnp.concatenate([upper_rows, lower_rows], axis=1)
    return columns.reshape(matrix.shape)


def solution(mesh):
    in_specs = (P("rows", "cols", None, None), P())
    out_specs = P("rows", "cols", None, None)
    return jax.shard_map(body, mesh=mesh, in_specs=in_specs, out_specs=out_specs, check_vma=False)
```

profile of v0, /device:TPU:0, one launch (start us, length us, event | category | flops | bytes accessed | tf_op | source)
XLA Modules:
  0.0 463.2 jit_solution(2592383849989567668)
XLA Ops:
  8.0 3.2 fusion.123
  24.4 92.0 %all-reduce.3.cloned.1.call-done = f32[8,256,256]{2,1,0:T(8,128)} async-done(((f32[8,256,256]{2,1,0:T(8,128)}), f32[8,256,256]{2,1,0:T(8,128)}) %all-reduce.3.cloned.1.call-update) | async-done | bytes 2097168 | tf_op jit(solution)/shard_map/psum | solution.py:49
  116.4 17.5 %copy.30 = f32[8,256,256]{0,2,1:T(8,128)} copy(f32[8,256,256]{2,1,0:T(8,128)} %all-reduce.3.cloned.1.call-done) | data formatting | bytes 4194304 | tf_op jit(solution)/shard_map/psum | solution.py:49
  133.9 2.3 gather_fusion
  138.7 3.5 fusion.22
  142.2 4.1 fusion.24
  146.3 3.3 multiply_reduce_fusion.6
  149.6 16.5 %copy.32 = f32[8,256,256]{0,2,1:T(8,128)} copy(f32[8,256,256]{1,2,0:T(8,128)S(1)} %get-tuple-element.56) | data formatting | bytes 4194304 | tf_op jit(solution)/shard_map/pji,pjk->pik/dot_general | solution.py:42
  166.1 2.3 gather_fusion.1
  170.1 5.1 %fusion.21 = f32[8,256,256]{1,2,0:T(8,128)S(1)} fusion(f32[8,256,256]{1,2,0:T(8,128)S(1)} %get-tuple-element.56, f32[8,256]{1,0:T(8,128)S(1)} %get-tuple-element.34, f32[256,256]{1,0:T(8,128)} %fusion.135, f32[8,256]{1,0:T(8,128)S(1)} %get-tuple-element.33, f32[256,256]{1,0:T(8,128)S(1)} %get-tuple-element.67), kind=kOutput, calls=%fused_computation.42 | convolution fusion | flops 1612185600 | bytes 4734976 | tf_op jit(solution)/shard_map/pij,pjk->pik/dot_general | solution.py:41
  175.2 3.3 multiply_reduce_fusion.5
  178.6 16.6 %copy.34 = f32[8,256,256]{0,2,1:T(8,128)} copy(f32[8,256,256]{1,2,0:T(8,128)S(1)} %get-tuple-element.58) | data formatting | bytes 4194304 | tf_op jit(solution)/shard_map/pji,pjk->pik/dot_general | solution.py:42
  195.2 2.3 gather_fusion.2
  199.3 5.1 %fusion.18 = f32[8,256,256]{1,2,0:T(8,128)S(1)} fusion(f32[8,256,256]{1,2,0:T(8,128)S(1)} %get-tuple-element.58, f32[8,256]{1,0:T(8,128)S(1)} %get-tuple-element.32, f32[256,256]{1,0:T(8,128)} %fusion.136, f32[8,256]{1,0:T(8,128)S(1)} %get-tuple-element.31, f32[256,256]{1,0:T(8,128)S(1)} %get-tuple-element.67), kind=kOutput, calls=%fused_computation.37 | convolution fusion | flops 1612185600 | bytes 4734976 | tf_op jit(solution)/shard_map/pij,pjk->pik/dot_general | solution.py:41
  204.4 3.3 multiply_reduce_fusion.4
  207.8 16.4 %copy.36 = f32[8,256,256]{0,2,1:T(8,128)} copy(f32[8,256,256]{1,2,0:T(8,128)S(1)} %get-tuple-element.60) | data formatting | bytes 4194304 | tf_op jit(solution)/shard_map/pji,pjk->pik/dot_general | solution.py:42
  224.2 2.3 gather_fusion.3
  228.2 5.1 %fusion.15 = f32[8,256,256]{1,2,0:T(8,128)S(1)} fusion(f32[8,256,256]{1,2,0:T(8,128)S(1)} %get-tuple-element.60, f32[8,256]{1,0:T(8,128)S(1)} %get-tuple-element.30, f32[256,256]{1,0:T(8,128)} %fusion.137, f32[8,256]{1,0:T(8,128)S(1)} %get-tuple-element.29, f32[256,256]{1,0:T(8,128)S(1)} %get-tuple-element.67), kind=kOutput, calls=%fused_computation.32 | convolution fusion | flops 1612185600 | bytes 4734976 | tf_op jit(solution)/shard_map/pij,pjk->pik/dot_general | solution.py:41
  233.3 2.6 fusion.14
  236.0 2.5 fusion.19
  238.5 2.7 fusion.16
  241.3 2.5 fusion.13
  243.8 2.4 convolution_bitcast_fusion.1
  246.2 2.1 reshape.365
  248.3 1.7 fusion.192
  252.7 3.1 collective-permute-done
  255.8 1.8 fusion.194
  259.6 70.2 %all-reduce.5.cloned.1.call-done = f32[8,128,128]{1,2,0:T(8,128)} async-done(((f32[8,128,128]{1,2,0:T(8,128)}), f32[8,128,128]{1,2,0:T(8,128)}) %all-reduce.5.cloned.1.call-update) | async-done | bytes 524304 | tf_op jit(solution)/shard_map/psum | solution.py:66
  331.9 1.7 maximum_maximum_fusion
  333.6 16.7 %copy.43 = f32[8,256,256]{0,2,1:T(8,128)} copy(f32[8,256,256]{1,2,0:T(8,128)S(1)} %get-tuple-element.5) | data formatting | bytes 4194304 | tf_op jit(solution)/shard_map/concatenate | solution.py:69
  350.3 2.4 gather_fusion.4
  353.1 3.5 fusion.12
  356.6 4.1 fusion.11
  360.7 2.7 multiply_reduce_fusion.2
  363.5 16.4 %copy.45 = f32[8,256,256]{0,2,1:T(8,128)} copy(f32[8,256,256]{1,2,0:T(8,128)S(1)} %get-tuple-element.62) | data formatting | bytes 4194304 | tf_op jit(solution)/shard_map/pji,pjk->pik/dot_general | solution.py:42
  380.0 2.3 gather_fusion.5
  382.6 4.1 fusion.8
  386.8 3.8 fusion.9
  390.5 2.7 multiply_reduce_fusion.1
  393.3 16.5 %copy.47 = f32[8,256,256]{0,2,1:T(8,128)} copy(f32[8,256,256]{1,2,0:T(8,128)S(1)} %get-tuple-element.64) | data formatting | bytes 4194304 | tf_op jit(solution)/shard_map/pji,pjk->pik/dot_general | solution.py:42
  409.8 2.3 gather_fusion.6
  412.5 4.1 fusion.5
  416.6 3.8 fusion.6
  420.4 2.7 multiply_reduce_fusion
  423.1 16.5 %copy.49 = f32[8,256,256]{0,2,1:T(8,128)} copy(f32[8,256,256]{1,2,0:T(8,128)S(1)} %get-tuple-element.66) | data formatting | bytes 4194304 | tf_op jit(solution)/shard_map/pji,pjk->pik/dot_general | solution.py:42
  439.6 2.3 gather_fusion.7
  442.3 4.1 fusion
  449.0 5.8 %collective-permute-done.2 = f32[64,8,128]{2,1,0:T(8,128)S(1)} collective-permute-done((f32[64,8,128]{2,1,0:T(8,128)S(1)}, f32[64,8,128]{2,1,0:T(8,128)S(1)}, u32[]{:S(2)}, u32[]{:S(2)}) %collective-permute-start.2) | collective-permute-done | bytes 262176 | tf_op jit(solution)/shard_map/ppermute | solution.py:12
  (156 shorter events, 34.0 us)
Async XLA Ops:
  6.5 109.9 %all-reduce.3.cloned.1.call-start = ((), (), s32[]{:S(2)}) async-start(), calls=%async_computation | async-start | bytes 4194304 | tf_op jit(solution)/shard_map/psum | solution.py:49
  8.0 3.5 copy-start.41
  11.2 318.5 %all-reduce.5.cloned.1.call-start = ((), (), s32[]{:S(2)}) async-start(), calls=%async_computation.1 | async-start | bytes 1048576 | tf_op jit(solution)/shard_map/psum | solution.py:66
  11.5 12.9 %copy-start.31 = (s32[1,1,256]{2,1,0:T(1,128)}, s32[1,1,256]{2,1,0:T(1,128)S(1)}, u32[]{:S(2)}) copy-start(s32[1,1,256]{2,1,0:T(1,128)S(1)} %get-tuple-element.22) | copy-start | bytes 3076
  11.5 12.9 %copy-start.33 = (s32[1,1,256]{2,1,0:T(1,128)}, s32[1,1,256]{2,1,0:T(1,128)S(1)}, u32[]{:S(2)}) copy-start(s32[1,1,256]{2,1,0:T(1,128)S(1)} %get-tuple-element.16) | copy-start | bytes 3076
  11.5 12.9 %copy-start.35 = (s32[1,1,256]{2,1,0:T(1,128)}, s32[1,1,256]{2,1,0:T(1,128)S(1)}, u32[]{:S(2)}) copy-start(s32[1,1,256]{2,1,0:T(1,128)S(1)} %get-tuple-element.21) | copy-start | bytes 3076
  11.5 12.9 %copy-start.37 = (s32[1,1,256]{2,1,0:T(1,128)}, s32[1,1,256]{2,1,0:T(1,128)S(1)}, u32[]{:S(2)}) copy-start(s32[1,1,256]{2,1,0:T(1,128)S(1)} %get-tuple-element.20) | copy-start | bytes 3076
  11.5 12.9 %copy-start.38 = (s32[1,1,256]{2,1,0:T(1,128)}, s32[1,1,256]{2,1,0:T(1,128)S(1)}, u32[]{:S(2)}) copy-start(s32[1,1,256]{2,1,0:T(1,128)S(1)} %get-tuple-element.19) | copy-start | bytes 3076
  11.5 12.9 %copy-start.39 = (s32[1,1,256]{2,1,0:T(1,128)}, s32[1,1,256]{2,1,0:T(1,128)S(1)}, u32[]{:S(2)}) copy-start(s32[1,1,256]{2,1,0:T(1,128)S(1)} %get-tuple-element.18) | copy-start | bytes 3076
  11.6 12.9 %copy-start.40 = (s32[1,1,256]{2,1,0:T(1,128)}, s32[1,1,256]{2,1,0:T(1,128)S(1)}, u32[]{:S(2)}) copy-start(s32[1,1,256]{2,1,0:T(1,128)S(1)} %get-tuple-element.17) | copy-start | bytes 3076
  116.4 19.9 %copy-start = (f32[8,256,256]{2,1,0:T(8,128)S(1)}, f32[8,256,256]{2,1,0:T(8,128)}, u32[]{:S(2)}) copy-start(f32[8,256,256]{2,1,0:T(8,128)} %all-reduce.3.cloned.1.call-done) | copy-start | bytes 6291460
  142.2 4.1 copy-start.22
  170.1 5.1 %copy-start.25 = (f32[8,256]{1,0:T(8,128)}, f32[8,256]{1,0:T(8,128)S(1)}, u32[]{:S(2)}) copy-start(f32[8,256]{1,0:T(8,128)S(1)} %get-tuple-element.34) | copy-start | bytes 24580
  170.1 5.1 %copy-start.4 = (f32[256,256]{1,0:T(8,128)S(1)}, f32[256,256]{1,0:T(8,128)}, u32[]{:S(2)}) copy-start(f32[256,256]{1,0:T(8,128)} %fusion.135) | copy-start | bytes 786436
  170.1 5.1 %copy-start.21 = (f32[256,256]{0,1:T(8,128)S(1)}, f32[256,256]{0,1:T(8,128)}, u32[]{:S(2)}) copy-start(f32[256,256]{0,1:T(8,128)} %fusion.130) | copy-start | bytes 786436
  199.2 5.2 %copy-start.27 = (f32[8,256]{1,0:T(8,128)}, f32[8,256]{1,0:T(8,128)S(1)}, u32[]{:S(2)}) copy-start(f32[8,256]{1,0:T(8,128)S(1)} %get-tuple-element.31) | copy-start | bytes 24580
  199.2 5.2 %copy-start.29 = (f32[8,256]{1,0:T(8,128)}, f32[8,256]{1,0:T(8,128)S(1)}, u32[]{:S(2)}) copy-start(f32[8,256]{1,0:T(8,128)S(1)} %get-tuple-element.32) | copy-start | bytes 24580
  199.2 5.2 %copy-start.6 = (f32[256,256]{1,0:T(8,128)S(1)}, f32[256,256]{1,0:T(8,128)}, u32[]{:S(2)}) copy-start(f32[256,256]{1,0:T(8,128)} %fusion.136) | copy-start | bytes 786436
  199.3 5.2 %copy-start.20 = (f32[256,256]{0,1:T(8,128)S(1)}, f32[256,256]{0,1:T(8,128)}, u32[]{:S(2)}) copy-start(f32[256,256]{0,1:T(8,128)} %fusion.129) | copy-start | bytes 786436
  228.2 5.1 %copy-start.8 = (f32[256,256]{1,0:T(8,128)S(1)}, f32[256,256]{1,0:T(8,128)}, u32[]{:S(2)}) copy-start(f32[256,256]{1,0:T(8,128)} %fusion.137) | copy-start | bytes 786436
  233.3 2.6 copy-start.1
  233.3 2.6 copy-start.5
  233.3 2.6 copy-start.26
  250.0 5.8 %collective-permute-start = (f32[64,8,128]{2,0,1:T(8,128)S(1)}, f32[64,8,128]{2,0,1:T(8,128)S(1)}, u32[]{:S(2)}, u32[]{:S(2)}) collective-permute-start(f32[64,8,128]{2,0,1:T(8,128)S(1)} %bitcast.109), channel_id=1, source_target_pairs={{3,0},{0,1},{1,2},{2,3},{7,4},{4,5},{5,6},{6,7},{11,8},{8,9},{9,10... | collective-permute-start | bytes 786440 | tf_op jit(solution)/shard_map/ppermute | solution.py:12
  251.1 79.9 %collective-permute-start.1 = (f32[8,128,128]{1,2,0:T(8,128)}, f32[8,128,128]{1,2,0:T(8,128)S(1)}, u32[]{:S(2)}, u32[]{:S(2)}) collective-permute-start(f32[8,128,128]{1,2,0:T(8,128)} %get-tuple-element.8), channel_id=1, source_target_pairs={{3,0},{0,1},{1,2},{2,3},{7,4},{4,5},{5,6},{6,7},{11,8},{8,9},{9,10... | collective-permute-start | bytes 1572872 | tf_op jit(solution)/shard_map/ppermute | solution.py:12
  331.0 2.6 copy-start.12
  333.6 19.2 %copy-start.36 = (s32[1,1,256]{2,1,0:T(1,128)S(1)}, s32[1,1,256]{2,1,0:T(1,128)}, u32[]{:S(2)}) copy-start(s32[1,1,256]{2,1,0:T(1,128)} %copy-done.35) | copy-start | bytes 3076
  333.6 19.2 %copy-start.46 = (f32[256]{0:T(256)S(1)}, f32[256]{0:T(256)}, u32[]{:S(2)}) copy-start(f32[256]{0:T(256)} %get-tuple-element.43) | copy-start | bytes 3076
  333.6 19.2 %copy-start.47 = (f32[256]{0:T(256)S(1)}, f32[256]{0:T(256)}, u32[]{:S(2)}) copy-start(f32[256]{0:T(256)} %get-tuple-element.44) | copy-start | bytes 3076
  333.6 19.5 %copy-start.10 = (f32[256,256]{1,0:T(8,128)S(1)}, f32[256,256]{1,0:T(8,128)}, u32[]{:S(2)}) copy-start(f32[256,256]{1,0:T(8,128)} %fusion.138) | copy-start | bytes 786436
  350.3 6.2 %copy-start.11 = (f32[8,128,128]{1,2,0:T(8,128)S(1)}, f32[8,128,128]{1,2,0:T(8,128)}, u32[]{:S(2)}) copy-start(f32[8,128,128]{1,2,0:T(8,128)} %all-reduce.5.cloned.1.call-done) | copy-start | bytes 1572868
  350.3 6.2 %copy-start.13 = (f32[8,128,128]{1,2,0:T(8,128)S(1)}, f32[8,128,128]{1,2,0:T(8,128)}, u32[]{:S(2)}) copy-start(f32[8,128,128]{1,2,0:T(8,128)} %copy-done.12) | copy-start | bytes 1572868
  350.3 6.2 %copy-start.14 = (f32[8,128,128]{1,2,0:T(8,128)S(1)}, f32[8,128,128]{1,2,0:T(8,128)}, u32[]{:S(2)}) copy-start(f32[8,128,128]{1,2,0:T(8,128)} %get-tuple-element.7) | copy-start | bytes 1572868
  350.3 6.2 %copy-start.24 = (f32[8,128,128]{1,2,0:T(8,128)S(1)}, f32[8,128,128]{1,2,0:T(8,128)}, u32[]{:S(2)}) copy-start(f32[8,128,128]{1,2,0:T(8,128)} %copy-done.23) | copy-start | bytes 1572868
  356.6 4.1 copy-start.18
  363.5 18.9 %copy-start.34 = (s32[1,1,256]{2,1,0:T(1,128)S(1)}, s32[1,1,256]{2,1,0:T(1,128)}, u32[]{:S(2)}) copy-start(s32[1,1,256]{2,1,0:T(1,128)} %copy-done.33) | copy-start | bytes 3076
  363.5 18.9 %copy-start.44 = (f32[256]{0:T(256)S(1)}, f32[256]{0:T(256)}, u32[]{:S(2)}) copy-start(f32[256]{0:T(256)} %get-tuple-element.41) | copy-start | bytes 3076
  363.5 18.8 %copy-start.45 = (f32[256]{0:T(256)S(1)}, f32[256]{0:T(256)}, u32[]{:S(2)}) copy-start(f32[256]{0:T(256)} %get-tuple-element.42) | copy-start | bytes 3076
  382.6 4.1 copy-start.2
  386.8 3.8 copy-start.17
  393.3 18.9 %copy-start.32 = (s32[1,1,256]{2,1,0:T(1,128)S(1)}, s32[1,1,256]{2,1,0:T(1,128)}, u32[]{:S(2)}) copy-start(s32[1,1,256]{2,1,0:T(1,128)} %copy-done.31) | copy-start | bytes 3076
  393.3 18.9 %copy-start.42 = (f32[256]{0:T(256)S(1)}, f32[256]{0:T(256)}, u32[]{:S(2)}) copy-start(f32[256]{0:T(256)} %get-tuple-element.39) | copy-start | bytes 3076
  393.3 18.9 %copy-start.43 = (f32[256]{0:T(256)S(1)}, f32[256]{0:T(256)}, u32[]{:S(2)}) copy-start(f32[256]{0:T(256)} %get-tuple-element.40) | copy-start | bytes 3076
  412.5 4.1 copy-start.3
  416.6 3.8 copy-start.16
  423.1 19.2 %copy-start.19 = (f32[256,256]{1,0:T(8,128)S(1)}, f32[256,256]{1,0:T(8,128)}, u32[]{:S(2)}) copy-start(f32[256,256]{1,0:T(8,128)} %fusion.141) | copy-start | bytes 786436
  442.3 4.2 copy-start.15
  449.0 5.8 %collective-permute-start.2 = (f32[64,8,128]{2,1,0:T(8,128)S(1)}, f32[64,8,128]{2,1,0:T(8,128)S(1)}, u32[]{:S(2)}, u32[]{:S(2)}) collective-permute-start(f32[64,8,128]{2,1,0:T(8,128)S(1)} %bitcast.108), channel_id=1, source_target_pairs={{3,0},{0,1},{1,2},{2,3},{7,4},{4,5},{5,6},{6,7},{11,8},{8,9},{9,10... | collective-permute-start | bytes 786440 | tf_op jit(solution)/shard_map/ppermute | solution.py:12
  (5 other events, 10.9 us)
Sparse Core Ops, SparseCore 0:
  11.4 105.0 all-reduce.2
  257.8 71.9 all-reduce.4
where the time goes:
time: 467 us; the launch traced here: 463 us
  waiting for transfers between devices  171 us (37%)
  local copies, waits for them, and re-layouts  165 us (35%)
  matrix products  92.9 us (20%)
  other arithmetic  18 us (4%)
  between operations  14.6 us (3%)
    dot_general x6, local copies, waits for them, and re-layouts, diagonalize(): jnp.einsum('pji,pjk->pik', rot_now, product, precision=lax.Precision.HIGH...  98.9 us
    psum x1, waiting for transfers between devices, full_grams(): return lax.psum(local_sum, 'rows')  92 us
    psum x1, waiting for transfers between devices, body(): cross = lax.psum(cross_local, 'rows')  70.2 us
    dot_general x7, matrix products, diagonalize(): jnp.einsum('pij,pjk->pik', grams, rot_now, precision=lax.Precision.HIGHEST)  31.7 us
    dot_general x8, matrix products, diagonalize(): jnp.einsum('pij,pjk->pik', rotation, rot_now, precision=lax.Precision.HIG...  26.3 us
    gather x16, local copies, waits for them, and re-layouts, diagonalize(): diagonal_now = jnp.diagonal(grams, axis1=1, axis2=2)  21 us
    dot_general x7, matrix products, diagonalize(): jnp.einsum('pji,pjk->pik', rot_now, product, precision=lax.Precision.HIGH...  20.8 us
    psum x1, local copies, waits for them, and re-layouts, full_grams(): return lax.psum(local_sum, 'rows')  17.5 us
  transfers between devices with their start and end apart: 5, of which 4 were waited for; matrix products, arithmetic and copies ran while one was open for 4% of the time, Pallas kernels for 0%

commit v1 on v0

--- a/solution.py
+++ b/solution.py
@@ -63,7 +63,9 @@
         columns = jnp.stack([tops, bottoms], axis=2).reshape(rows_here, pair_here, halves * width)
         if step_index + 1 < STEPS:
             cross_local = jnp.einsum("mpi,mpj->pij", tops, bottoms, precision=lax.Precision.HIGHEST)
-            cross = lax.psum(cross_local, "rows")
+            cross = cross_local
+            for hop in (1, 2, 4):
+                cross = cross + lax.ppermute(cross, "rows", [(dev, dev ^ hop) for dev in range(8)])
             upper_rows = jnp.concatenate([grams[:, :width, :width], cross], axis=2)
             lower_rows = jnp.concatenate([jnp.swapaxes(cross, 1, 2), low_grams], axis=2)
             grams = jnp.concatenate([upper_rows, lower_rows], axis=1)

time: 467 us -> 438 us (0.938)
  waiting for transfers between devices: 171 us -> 139 us
    psum x1 -> x0, waiting for transfers between devices: 70.2 us -> none  [body(): cross = lax.psum(cross_local, 'rows')]
    ppermute x0 -> x3, waiting for transfers between devices: none -> 34.2 us  [body(): lax.ppermute(cross, 'rows', [(dev, dev ^ hop) for dev in range(8)])]
  transfers between devices with their start and end apart: 5 -> 7, of which waited for: 4 -> 6; matrix products, arithmetic and copies ran while one was open for 4% -> 5% of each run, Pallas kernels for 0% -> 0%
where the time goes in v1:
time: 438 us; the launch traced here: 435 us
  local copies, waits for them, and re-layouts  166 us (38%)
  waiting for transfers between devices  139 us (32%)
  matrix products  92.6 us (21%)
  other arithmetic  17.1 us (4%)
  between operations  14.6 us (3%)
  starting transfers between devices  5.2 us (1%)
    dot_general x6, local copies, waits for them, and re-layouts, diagonalize(): jnp.einsum('pji,pjk->pik', rot_now, product, precision=lax.Precision.HIGH...  101 us
    psum x1, waiting for transfers between devices, full_grams(): return lax.psum(local_sum, 'rows')  94.1 us
    ppermute x3, waiting for transfers between devices, body(): lax.ppermute(cross, 'rows', [(dev, dev ^ hop) for dev in range(8)])  34.2 us
    dot_general x7, matrix products, diagonalize(): jnp.einsum('pij,pjk->pik', grams, rot_now, precision=lax.Precision.HIGHEST)  30.7 us
    dot_general x8, matrix products, diagonalize(): jnp.einsum('pij,pjk->pik', rotation, rot_now, precision=lax.Precision.HIG...  28.6 us
    gather x16, local copies, waits for them, and re-layouts, diagonalize(): diagonal_now = jnp.diagonal(grams, axis1=1, axis2=2)  20.9 us
    dot_general x7, matrix products, diagonalize(): jnp.einsum('pji,pjk->pik', rot_now, product, precision=lax.Precision.HIGH...  20.8 us
    psum x1, local copies, waits for them, and re-layouts, full_grams(): return lax.psum(local_sum, 'rows')  17.7 us
  transfers between devices with their start and end apart: 7, of which 6 were waited for; matrix products, arithmetic and copies ran while one was open for 5% of the time, Pallas kernels for 0%

profile of v1, /device:TPU:0, one launch (start us, length us, event | category | flops | bytes accessed | tf_op | source)
XLA Modules:
  0.0 434.6 jit_solution(7016972761893894517)
XLA Ops:
  8.0 3.2 fusion.123
  22.4 94.1 %all-reduce.2.cloned.1.call-done = f32[8,256,256]{2,1,0:T(8,128)} async-done(((f32[8,256,256]{2,1,0:T(8,128)}), f32[8,256,256]{2,1,0:T(8,128)}) %all-reduce.2.cloned.1.call-update) | async-done | bytes 2097168 | tf_op jit(solution)/shard_map/psum | solution.py:49
  116.5 17.7 %copy.31 = f32[8,256,256]{0,2,1:T(8,128)} copy(f32[8,256,256]{2,1,0:T(8,128)} %all-reduce.2.cloned.1.call-done) | data formatting | bytes 4194304 | tf_op jit(solution)/shard_map/psum | solution.py:49
  134.2 2.3 gather_fusion
  139.0 3.5 fusion.22
  142.5 4.1 fusion.24
  146.5 3.3 multiply_reduce_fusion.6
  149.9 16.7 %copy.33 = f32[8,256,256]{0,2,1:T(8,128)} copy(f32[8,256,256]{1,2,0:T(8,128)S(1)} %get-tuple-element.56) | data formatting | bytes 4194304 | tf_op jit(solution)/shard_map/pji,pjk->pik/dot_general | solution.py:42
  166.6 2.3 gather_fusion.1
  170.6 5.1 %fusion.21 = f32[8,256,256]{1,2,0:T(8,128)S(1)} fusion(f32[8,256,256]{1,2,0:T(8,128)S(1)} %get-tuple-element.56, f32[8,256]{1,0:T(8,128)S(1)} %get-tuple-element.34, f32[256,256]{1,0:T(8,128)} %fusion.135, f32[8,256]{1,0:T(8,128)S(1)} %get-tuple-element.33, f32[256,256]{1,0:T(8,128)S(1)} %get-tuple-element.67), kind=kOutput, calls=%fused_computation.42 | convolution fusion | flops 1612185600 | bytes 4734976 | tf_op jit(solution)/shard_map/pij,pjk->pik/dot_general | solution.py:41
  175.8 3.3 multiply_reduce_fusion.5
  179.1 16.9 %copy.35 = f32[8,256,256]{0,2,1:T(8,128)} copy(f32[8,256,256]{1,2,0:T(8,128)S(1)} %get-tuple-element.58) | data formatting | bytes 4194304 | tf_op jit(solution)/shard_map/pji,pjk->pik/dot_general | solution.py:42
  196.0 2.3 gather_fusion.2
  200.1 5.1 %fusion.18 = f32[8,256,256]{1,2,0:T(8,128)S(1)} fusion(f32[8,256,256]{1,2,0:T(8,128)S(1)} %get-tuple-element.58, f32[8,256]{1,0:T(8,128)S(1)} %get-tuple-element.32, f32[256,256]{1,0:T(8,128)} %fusion.136, f32[8,256]{1,0:T(8,128)S(1)} %get-tuple-element.31, f32[256,256]{1,0:T(8,128)S(1)} %get-tuple-element.67), kind=kOutput, calls=%fused_computation.37 | convolution fusion | flops 1612185600 | bytes 4734976 | tf_op jit(solution)/shard_map/pij,pjk->pik/dot_general | solution.py:41
  205.2 3.3 multiply_reduce_fusion.4
  208.6 16.7 %copy.37 = f32[8,256,256]{0,2,1:T(8,128)} copy(f32[8,256,256]{1,2,0:T(8,128)S(1)} %get-tuple-element.60) | data formatting | bytes 4194304 | tf_op jit(solution)/shard_map/pji,pjk->pik/dot_general | solution.py:42
  225.3 2.3 gather_fusion.3
  228.3 4.1 fusion.19
  232.5 2.5 fusion.16
  235.3 2.5 fusion.13
  237.8 2.4 convolution_bitcast_fusion.1
  240.3 2.2 reshape.365
  245.2 5.0 %collective-permute-done = f32[64,8,128]{2,0,1:T(8,128)S(1)} collective-permute-done((f32[64,8,128]{2,0,1:T(8,128)S(1)}, f32[64,8,128]{2,0,1:T(8,128)S(1)}, u32[]{:S(2)}, u32[]{:S(2)}) %collective-permute-start) | collective-permute-done | bytes 262176 | tf_op jit(solution)/shard_map/ppermute | solution.py:12
  252.7 4.1 fusion.15
  256.8 7.4 %collective-permute-done.1 = f32[8,128,128]{1,2,0:T(8,128)S(1)} collective-permute-done((f32[8,128,128]{1,2,0:T(8,128)S(1)}, f32[8,128,128]{1,2,0:T(8,128)S(1)}, u32[]{:S(2)}, u32[]{:S(2)}) %collective-permute-start.1) | collective-permute-done | bytes 524320 | tf_op jit(solution)/shard_map/ppermute | solution.py:68
  265.4 2.6 fusion.14
  269.3 7.1 %collective-permute-done.2 = f32[8,128,128]{1,2,0:T(8,128)S(1)} collective-permute-done((f32[8,128,128]{1,2,0:T(8,128)S(1)}, f32[8,128,128]{1,2,0:T(8,128)S(1)}, u32[]{:S(2)}, u32[]{:S(2)}) %collective-permute-start.2) | collective-permute-done | bytes 524320 | tf_op jit(solution)/shard_map/ppermute | solution.py:68
  276.5 1.8 collective-permute-start.3
  280.1 19.8 %collective-permute-done.3 = f32[8,128,128]{1,2,0:T(8,128)S(1)} collective-permute-done((f32[8,128,128]{1,2,0:T(8,128)S(1)}, f32[8,128,128]{1,2,0:T(8,128)S(1)}, u32[]{:S(2)}, u32[]{:S(2)}) %collective-permute-start.3) | collective-permute-done | bytes 524320 | tf_op jit(solution)/shard_map/ppermute | solution.py:68
  303.6 16.6 %copy.45 = f32[8,256,256]{0,2,1:T(8,128)} copy(f32[8,256,256]{1,2,0:T(8,128)S(1)} %get-tuple-element.5) | data formatting | bytes 4194304 | tf_op jit(solution)/shard_map/concatenate | solution.py:71
  320.1 2.3 gather_fusion.4
  322.8 4.4 %fusion.12 = f32[8,256,256]{2,1,0:T(8,128)} fusion(f32[8,256]{1,0:T(8,128)S(1)} %get-tuple-element.28, f32[256,256]{1,0:T(8,128)} %fusion.138, f32[8,256]{1,0:T(8,128)S(1)} %get-tuple-element.27, f32[256,256]{1,0:T(8,128)S(1)} %get-tuple-element.67), kind=kOutput, calls=%fused_computation.27 | convolution fusion | flops 1612185600 | bytes 2637824 | tf_op jit(solution)/shard_map/pij,pjk->pik/dot_general | solution.py:43
  327.3 4.1 fusion.11
  331.4 2.8 multiply_reduce_fusion.2
  334.2 16.7 %copy.47 = f32[8,256,256]{0,2,1:T(8,128)} copy(f32[8,256,256]{1,2,0:T(8,128)S(1)} %get-tuple-element.62) | data formatting | bytes 4194304 | tf_op jit(solution)/shard_map/pji,pjk->pik/dot_general | solution.py:42
  350.9 2.3 gather_fusion.5
  353.6 4.1 fusion.8
  357.7 3.8 fusion.9
  361.4 2.7 multiply_reduce_fusion.1
  364.2 16.7 %copy.49 = f32[8,256,256]{0,2,1:T(8,128)} copy(f32[8,256,256]{1,2,0:T(8,128)S(1)} %get-tuple-element.64) | data formatting | bytes 4194304 | tf_op jit(solution)/shard_map/pji,pjk->pik/dot_general | solution.py:42
  380.9 2.3 gather_fusion.6
  383.6 4.1 fusion.5
  387.7 3.8 fusion.6
  391.5 2.7 multiply_reduce_fusion
  394.2 16.8 %copy.51 = f32[8,256,256]{0,2,1:T(8,128)} copy(f32[8,256,256]{1,2,0:T(8,128)S(1)} %get-tuple-element.66) | data formatting | bytes 4194304 | tf_op jit(solution)/shard_map/pji,pjk->pik/dot_general | solution.py:42
  411.0 2.3 gather_fusion.7
  413.7 4.1 fusion
  420.4 5.8 %collective-permute-done.5 = f32[64,8,128]{2,1,0:T(8,128)S(1)} collective-permute-done((f32[64,8,128]{2,1,0:T(8,128)S(1)}, f32[64,8,128]{2,1,0:T(8,128)S(1)}, u32[]{:S(2)}, u32[]{:S(2)}) %collective-permute-start.5) | collective-permute-done | bytes 262176 | tf_op jit(solution)/shard_map/ppermute | solution.py:12
  (164 shorter events, 37.9 us)
Async XLA Ops:
  6.5 109.9 %all-reduce.2.cloned.1.call-start = ((), (), s32[]{:S(2)}) async-start(), calls=%async_computation | async-start | bytes 4194304 | tf_op jit(solution)/shard_map/psum | solution.py:49
  8.0 3.3 copy-start.44
  11.3 122.9 %copy-start.32 = (s32[1,1,256]{2,1,0:T(1,128)}, s32[1,1,256]{2,1,0:T(1,128)S(1)}, u32[]{:S(2)}) copy-start(s32[1,1,256]{2,1,0:T(1,128)S(1)} %get-tuple-element.22) | copy-start | bytes 3076
  11.3 122.9 %copy-start.34 = (s32[1,1,256]{2,1,0:T(1,128)}, s32[1,1,256]{2,1,0:T(1,128)S(1)}, u32[]{:S(2)}) copy-start(s32[1,1,256]{2,1,0:T(1,128)S(1)} %get-tuple-element.16) | copy-start | bytes 3076
  11.3 122.8 %copy-start.36 = (s32[1,1,256]{2,1,0:T(1,128)}, s32[1,1,256]{2,1,0:T(1,128)S(1)}, u32[]{:S(2)}) copy-start(s32[1,1,256]{2,1,0:T(1,128)S(1)} %get-tuple-element.21) | copy-start | bytes 3076
  11.3 122.8 %copy-start.38 = (s32[1,1,256]{2,1,0:T(1,128)}, s32[1,1,256]{2,1,0:T(1,128)S(1)}, u32[]{:S(2)}) copy-start(s32[1,1,256]{2,1,0:T(1,128)S(1)} %get-tuple-element.20) | copy-start | bytes 3076
  11.3 122.8 %copy-start.40 = (s32[1,1,256]{2,1,0:T(1,128)}, s32[1,1,256]{2,1,0:T(1,128)S(1)}, u32[]{:S(2)}) copy-start(s32[1,1,256]{2,1,0:T(1,128)S(1)} %get-tuple-element.19) | copy-start | bytes 3076
  11.3 122.8 %copy-start.41 = (s32[1,1,256]{2,1,0:T(1,128)}, s32[1,1,256]{2,1,0:T(1,128)S(1)}, u32[]{:S(2)}) copy-start(s32[1,1,256]{2,1,0:T(1,128)S(1)} %get-tuple-element.18) | copy-start | bytes 3076
  11.3 122.8 %copy-start.42 = (s32[1,1,256]{2,1,0:T(1,128)}, s32[1,1,256]{2,1,0:T(1,128)S(1)}, u32[]{:S(2)}) copy-start(s32[1,1,256]{2,1,0:T(1,128)S(1)} %get-tuple-element.17) | copy-start | bytes 3076
  116.5 20.1 %copy-start = (f32[8,256,256]{2,1,0:T(8,128)S(1)}, f32[8,256,256]{2,1,0:T(8,128)}, u32[]{:S(2)}) copy-start(f32[8,256,256]{2,1,0:T(8,128)} %all-reduce.2.cloned.1.call-done) | copy-start | bytes 6291460
  142.5 4.1 copy-start.20
  170.6 5.1 %copy-start.25 = (f32[8,256]{1,0:T(8,128)}, f32[8,256]{1,0:T(8,128)S(1)}, u32[]{:S(2)}) copy-start(f32[8,256]{1,0:T(8,128)S(1)} %get-tuple-element.34) | copy-start | bytes 24580
  170.6 5.1 %copy-start.5 = (f32[256,256]{1,0:T(8,128)S(1)}, f32[256,256]{1,0:T(8,128)}, u32[]{:S(2)}) copy-start(f32[256,256]{1,0:T(8,128)} %fusion.135) | copy-start | bytes 786436
  170.6 5.1 %copy-start.19 = (f32[256,256]{0,1:T(8,128)S(1)}, f32[256,256]{0,1:T(8,128)}, u32[]{:S(2)}) copy-start(f32[256,256]{0,1:T(8,128)} %fusion.130) | copy-start | bytes 786436
  200.0 5.2 %copy-start.26 = (f32[8,256]{1,0:T(8,128)}, f32[8,256]{1,0:T(8,128)S(1)}, u32[]{:S(2)}) copy-start(f32[8,256]{1,0:T(8,128)S(1)} %get-tuple-element.31) | copy-start | bytes 24580
  200.0 5.2 %copy-start.28 = (f32[8,256]{1,0:T(8,128)}, f32[8,256]{1,0:T(8,128)S(1)}, u32[]{:S(2)}) copy-start(f32[8,256]{1,0:T(8,128)S(1)} %get-tuple-element.32) | copy-start | bytes 24580
  200.1 5.2 %copy-start.6 = (f32[256,256]{1,0:T(8,128)S(1)}, f32[256,256]{1,0:T(8,128)}, u32[]{:S(2)}) copy-start(f32[256,256]{1,0:T(8,128)} %fusion.136) | copy-start | bytes 786436
  200.1 5.2 %copy-start.18 = (f32[256,256]{0,1:T(8,128)S(1)}, f32[256,256]{0,1:T(8,128)}, u32[]{:S(2)}) copy-start(f32[256,256]{0,1:T(8,128)} %fusion.129) | copy-start | bytes 786436
  228.3 4.1 copy-start.7
  228.3 4.1 copy-start.27
  228.3 4.1 copy-start.29
  232.4 2.6 copy-start.30
  232.5 2.9 copy-start.3
  237.8 6.6 %copy-start.35 = (s32[1,1,256]{2,1,0:T(1,128)S(1)}, s32[1,1,256]{2,1,0:T(1,128)}, u32[]{:S(2)}) copy-start(s32[1,1,256]{2,1,0:T(1,128)} %copy-done.34) | copy-start | bytes 3076
  240.2 12.5 %copy-start.33 = (s32[1,1,256]{2,1,0:T(1,128)S(1)}, s32[1,1,256]{2,1,0:T(1,128)}, u32[]{:S(2)}) copy-start(s32[1,1,256]{2,1,0:T(1,128)} %copy-done.32) | copy-start | bytes 3076
  240.3 12.5 %copy-start.4 = (f32[256,256]{1,0:T(8,128)S(1)}, f32[256,256]{1,0:T(8,128)}, u32[]{:S(2)}) copy-start(f32[256,256]{1,0:T(8,128)} %fusion.137) | copy-start | bytes 786436
  240.3 12.5 %copy-start.24 = (f32[8,256]{1,0:T(8,128)S(1)}, f32[8,256]{1,0:T(8,128)}, u32[]{:S(2)}) copy-start(f32[8,256]{1,0:T(8,128)} %copy-done.23) | copy-start | bytes 24580
  244.1 6.1 %collective-permute-start = (f32[64,8,128]{2,0,1:T(8,128)S(1)}, f32[64,8,128]{2,0,1:T(8,128)S(1)}, u32[]{:S(2)}, u32[]{:S(2)}) collective-permute-start(f32[64,8,128]{2,0,1:T(8,128)S(1)} %bitcast.109), channel_id=1, source_target_pairs={{3,0},{0,1},{1,2},{2,3},{7,4},{4,5},{5,6},{6,7},{11,8},{8,9},{9,10... | collective-permute-start | bytes 786440 | tf_op jit(solution)/shard_map/ppermute | solution.py:12
  251.2 13.0 %collective-permute-start.1 = (f32[8,128,128]{1,2,0:T(8,128)S(1)}, f32[8,128,128]{1,2,0:T(8,128)S(1)}, u32[]{:S(2)}, u32[]{:S(2)}) collective-permute-start(f32[8,128,128]{1,2,0:T(8,128)S(1)} %fusion.194), channel_id=1, source_target_pairs={{0,4},{4,0},{8,12},{12,8},{16,20},{20,16},{24,28},{28,24},{1,5},{5... | collective-permute-start | bytes 1572872 | tf_op jit(solution)/shard_map/ppermute | solution.py:68
  264.3 12.1 %collective-permute-start.2 = (f32[8,128,128]{1,2,0:T(8,128)S(1)}, f32[8,128,128]{1,2,0:T(8,128)S(1)}, u32[]{:S(2)}, u32[]{:S(2)}) collective-permute-start(f32[8,128,128]{1,2,0:T(8,128)S(1)} %add.141), channel_id=1, source_target_pairs={{0,8},{4,12},{8,0},{12,4},{16,24},{20,28},{24,16},{28,20},{1,9},{5... | collective-permute-start | bytes 1572872 | tf_op jit(solution)/shard_map/ppermute | solution.py:68
  268.9 32.0 %collective-permute-start.4 = (f32[8,128,128]{1,2,0:T(8,128)S(1)}, f32[8,128,128]{1,2,0:T(8,128)S(1)}, u32[]{:S(2)}, u32[]{:S(2)}) collective-permute-start(f32[8,128,128]{1,2,0:T(8,128)S(1)} %get-tuple-element.8), channel_id=1, source_target_pairs={{3,0},{0,1},{1,2},{2,3},{7,4},{4,5},{5,6},{6,7},{11,8},{8,9},{9,10... | collective-permute-start | bytes 1572872 | tf_op jit(solution)/shard_map/ppermute | solution.py:12
  276.5 23.4 %collective-permute-start.3 = (f32[8,128,128]{1,2,0:T(8,128)S(1)}, f32[8,128,128]{1,2,0:T(8,128)S(1)}, u32[]{:S(2)}, u32[]{:S(2)}) collective-permute-start(f32[8,128,128]{1,2,0:T(8,128)S(1)} %add.142), channel_id=1, source_target_pairs={{0,16},{4,20},{8,24},{12,28},{16,0},{20,4},{24,8},{28,12},{1,17},{... | collective-permute-start | bytes 1572872 | tf_op jit(solution)/shard_map/ppermute | solution.py:68
  303.5 19.0 %copy-start.37 = (s32[1,1,256]{2,1,0:T(1,128)S(1)}, s32[1,1,256]{2,1,0:T(1,128)}, u32[]{:S(2)}) copy-start(s32[1,1,256]{2,1,0:T(1,128)} %copy-done.36) | copy-start | bytes 3076
  303.5 19.0 %copy-start.45 = (f32[256]{0:T(256)S(1)}, f32[256]{0:T(256)}, u32[]{:S(2)}) copy-start(f32[256]{0:T(256)} %get-tuple-element.43) | copy-start | bytes 3076
  303.5 19.0 %copy-start.46 = (f32[256]{0:T(256)S(1)}, f32[256]{0:T(256)}, u32[]{:S(2)}) copy-start(f32[256]{0:T(256)} %get-tuple-element.44) | copy-start | bytes 3076
  320.1 7.1 %copy-start.9 = (f32[256,256]{1,0:T(8,128)S(1)}, f32[256,256]{1,0:T(8,128)}, u32[]{:S(2)}) copy-start(f32[256,256]{1,0:T(8,128)} %fusion.138) | copy-start | bytes 786436
  320.1 7.1 %copy-start.11 = (f32[8,128,128]{1,2,0:T(8,128)S(1)}, f32[8,128,128]{1,2,0:T(8,128)}, u32[]{:S(2)}) copy-start(f32[8,128,128]{1,2,0:T(8,128)} %copy.44) | copy-start | bytes 1572868
  320.1 7.1 %copy-start.12 = (f32[8,128,128]{1,2,0:T(8,128)S(1)}, f32[8,128,128]{1,2,0:T(8,128)}, u32[]{:S(2)}) copy-start(f32[8,128,128]{1,2,0:T(8,128)} %get-tuple-element.7) | copy-start | bytes 1572868
  320.1 7.1 %copy-start.22 = (f32[8,128,128]{1,2,0:T(8,128)S(1)}, f32[8,128,128]{1,2,0:T(8,128)}, u32[]{:S(2)}) copy-start(f32[8,128,128]{1,2,0:T(8,128)} %copy-done.21) | copy-start | bytes 1572868
  327.2 4.1 copy-start.10
  327.3 4.1 copy-start.15
  353.6 4.1 copy-start.1
  357.7 3.8 copy-start.14
  383.6 4.1 copy-start.2
  387.7 3.8 copy-start.16
  394.2 19.5 %copy-start.17 = (f32[256,256]{1,0:T(8,128)S(1)}, f32[256,256]{1,0:T(8,128)}, u32[]{:S(2)}) copy-start(f32[256,256]{1,0:T(8,128)} %fusion.141) | copy-start | bytes 786436
  413.7 4.2 copy-start.13
  420.3 5.8 %collective-permute-start.5 = (f32[64,8,128]{2,1,0:T(8,128)S(1)}, f32[64,8,128]{2,1,0:T(8,128)S(1)}, u32[]{:S(2)}, u32[]{:S(2)}) collective-permute-start(f32[64,8,128]{2,1,0:T(8,128)S(1)} %bitcast.108), channel_id=1, source_target_pairs={{3,0},{0,1},{1,2},{2,3},{7,4},{4,5},{5,6},{6,7},{11,8},{8,9},{9,10... | collective-permute-start | bytes 786440 | tf_op jit(solution)/shard_map/ppermute | solution.py:12
  (8 other events, 17.4 us)
Sparse Core Ops, SparseCore 0:
  11.4 105.0 all-reduce.1
